TPU v7x, 512 devices: a 4x2x32 block of a 4x8x32 slice. The times are simulated.
512 devices in a mesh: groups: 2 (over y), ep: 32 (over z), tp: 4 (over x), dp: 2 (over core).
Axes of the slice: x: 4, y: 2, z: 32, core: 2. Of those that a mesh axis runs over, the one named last changes fastest.
The devices are a block of a 4x8x32 slice.
Arguments:
- tokens: bfloat16 [8192, 1536], P(('groups', 'ep', 'tp', 'dp')), parts along dimension 0, may hold values from -6 to 6
- expert_ids: int32 [8192, 4], P(('groups', 'ep', 'tp', 'dp')), parts along dimension 0, may hold values from 0 to 63, all different within a row; in each aligned block of 16 rows (0 to 15, 16 to 31, ...) at most 2 rows name the same one
- gate_weights: float32 [8192, 4], P(('groups', 'ep', 'tp', 'dp')), parts along dimension 0, may hold values from 0.1 to 1
- w_gate: bfloat16 [64, 1536, 1536], P(('ep', 'dp'), None, 'tp'), may hold values from -0.15625 to 0.15625
- w_up: bfloat16 [64, 1536, 1536], P(('ep', 'dp'), None, 'tp'), may hold values from -0.15625 to 0.15625
- w_down: bfloat16 [64, 1536, 1536], P(('ep', 'dp'), None, 'tp'), may hold values from -0.15625 to 0.15625
Outputs:
- mixed: bfloat16 [8192, 1536], P(('groups', 'ep', 'tp', 'dp')), parts along dimension 0
- expert_loads: int32 [128], P('groups'), parts along dimension 0
There are 2 independent parts, one for each index of `groups`. A program takes and returns all parts, laid end to end along the dimension named above; an argument that names none is the same for every part. Nothing has to cross between parts.
Inputs may be any that keep to these rules, and one draw needn't show every extreme that they name: `expert_ids`: each row names 4 different experts. In each aligned block of 16 rows (the rows of one device) no expert is named by more than 2 rows, and in some blocks one expert is named by exactly 2 rows.
All inputs are finite; a program needn't handle non-finite values.
Results may differ from a plain program's by a relative error of at most 0.0057.
Values may be sent and summed in bfloat16 or wider, within the bound.
A program may use at most 64 MiB of HBM per device.

v0:
```python
import jax
import jax.numpy as jnp
from jax import lax
from jax.sharding import PartitionSpec as P


def one_axis_at_a_time(array, axes):
    for axis in axes:
        array = lax.psum(array, axis)
    return array


def copy_for_each(array, axis):
    copies = jnp.broadcast_to(array, (lax.axis_size(axis), *array.shape))
    return lax.all_to_all(copies, axis, split_axis=0, concat_axis=0, tiled=True)


def laid_out(blocks, dim):
    shape = list(blocks.shape[1:])
    shape[dim] *= blocks.shape[0]
    return jnp.moveaxis(blocks, 0, dim).reshape(shape)


def collect(array, axis, dim):
    blocks = copy_for_each(array, axis)
    return laid_out(blocks, dim)


def split_up(array, dim, size):
    before, after = (array.shape[:dim], array.shape[dim + 1 :])
    return jnp.moveaxis(array.reshape(*before, size, -1, *after), dim, 0)


def sent_and_summed(array, axis, dim):
    blocks = split_up(array, dim, lax.axis_size(axis))
    arrived = lax.all_to_all(blocks, axis, split_axis=0, concat_axis=0, tiled=True)
    return arrived.sum(axis=0)


def expert_apply(token_rows, gate_part, up_part, down_part):
    gate_value = jnp.dot(token_rows, gate_part, preferred_element_type=jnp.float32)
    up_value = jnp.dot(token_rows, up_part, preferred_element_type=jnp.float32)
    hidden = (jax.nn.silu(gate_value) * up_value).astype(jnp.bfloat16)
    return lax.dot_general(
        hidden, down_part, (((1,), (1,)), ((), ())), preferred_element_type=jnp.float32
    )


def per_device(tokens, expert_ids, gate_weights, w_gate, w_up, w_down):
    tok_rows = tokens.shape[0]
    model_width = tokens.shape[1]
    top_count = expert_ids.shape[1]
    ep_count = lax.axis_size("ep")
    dp_count = lax.axis_size("dp")
    experts = ep_count * dp_count
    capacity = max(2, 2 * tok_rows * top_count // experts)
    pair_ids = expert_ids.reshape(-1)
    expert_range = jnp.arange(experts, dtype=jnp.int32)
    onehot = (pair_ids[:, None] == expert_range[None, :]).astype(jnp.int32)
    local_counts = jnp.sum(onehot, axis=0).astype(jnp.float32)
    expert_loads = one_axis_at_a_time(local_counts, ("ep", "tp", "dp")).astype(jnp.int32)
    earlier = (jnp.cumsum(onehot, axis=0) - onehot) * onehot
    slot_ranks = jnp.sum(earlier, axis=1)
    targets = pair_ids * capacity + slot_ranks
    slot_range = jnp.arange(experts * capacity, dtype=jnp.int32)
    selector = jnp.any(
        targets.reshape(tok_rows, top_count)[None, :, :] == slot_range[:, None, None], axis=2
    )
    outgoing = jnp.dot(selector.astype(jnp.bfloat16), tokens, preferred_element_type=jnp.float32)
    outgoing = outgoing.astype(jnp.bfloat16).reshape(experts, capacity, model_width)
    arrived = lax.all_to_all(outgoing, ("ep", "dp"), split_axis=0, concat_axis=0, tiled=True)
    gate_local = w_gate[0]
    up_local = w_up[0]
    down_local = w_down[0]
    fragment = collect(arrived, "tp", 0)
    flat_rows = fragment.reshape(-1, model_width)
    partial_value = expert_apply(flat_rows, gate_local, up_local, down_local)
    partial_terms = partial_value.reshape(fragment.shape[0], capacity, model_width)
    finished = sent_and_summed(partial_terms, "tp", 0).astype(jnp.bfloat16)
    returned = lax.all_to_all(finished, ("ep", "dp"), split_axis=0, concat_axis=0, tiled=True)
    returned = returned.reshape(experts * capacity, model_width)
    picked = jnp.take(returned, targets, axis=0).reshape(tok_rows, top_count, model_width)
    mixed = jnp.sum(gate_weights[:, :, None] * picked.astype(jnp.float32), axis=1)
    return (mixed.astype(jnp.bfloat16), expert_loads)


def solution(mesh):
    return jax.shard_map(
        per_device,
        mesh=mesh,
        in_specs=(
            P(("groups", "ep", "tp", "dp"), None),
            P(("groups", "ep", "tp", "dp"), None),
            P(("groups", "ep", "tp", "dp"), None),
            P(("ep", "dp"), None, "tp"),
            P(("ep", "dp"), None, "tp"),
            P(("ep", "dp"), None, "tp"),
        ),
        out_specs=(P(("groups", "ep", "tp", "dp"), None), P("groups")),
        check_vma=False,
    )
```

profile of v0, /device:TPU:40, one launch (start us, length us, event | category | flops | bytes accessed | tf_op | source)
XLA Modules:
  0.0 284.0 jit_solution(17129399234200269265)
XLA Ops:
  0.6 0.9 copy.27
  1.7 0.1 reduce_window_sum.11
  1.8 0.2 fusion.9
  2.2 1.1 convolution_convert_fusion
  3.3 0.1 reshape.65
  3.5 100.1 %all_to_all.20 = bf16[64,2,1536]{2,1,0:T(2,128)(2,1)S(1)} all-to-all(bf16[64,2,1536]{2,1,0:T(2,128)(2,1)S(1)} %reshape.65), channel_id=1, replica_groups=mesh['groups'=2,'ep'=32,'tp'=4,'dp'=2] {'ep','dp'}, dimensions={0} | all-to-all | bytes 786432 | tf_op jit(solution)/shard_map/all_to_all | solution.py:71
  103.6 0.8 broadcast_in_dim.17
  104.4 24.0 %all_to_all.21 = bf16[4,64,2,1536]{3,2,1,0:T(2,128)(2,1)S(1)} all-to-all(bf16[4,64,2,1536]{3,2,1,0:T(2,128)(2,1)S(1)} %broadcast_in_dim.17), channel_id=1, replica_groups=mesh['groups'=2,'ep'=32,'tp'=4,'dp'=2] {'tp'}, dimensions={0} | all-to-all | bytes 3145728 | tf_op jit(solution)/shard_map/all_to_all | solution.py:15
  128.4 1.5 reshape_reshape.4
  129.9 2.9 %fusion.4 = f32[512,384]{1,0:T(8,128)S(1)} fusion(bf16[512,1536]{1,0:T(8,128)(2,1)} %reshape_reshape.4, bf16[1,1536,384]{2,1,0:T(8,128)(2,1)} %param.9), kind=kOutput, calls=%fused_computation.7 | convolution fusion | flops 603979776 | bytes 3538944 | tf_op jit(solution)/shard_map/dot_general | solution.py:41
  132.8 1.0 fusion
  133.8 0.1 dot_general.17
  134.0 1.0 fusion.1
  135.0 38.7 %all_to_all.22 = f32[4,64,2,1536]{3,1,2,0:T(8,128)} all-to-all(f32[4,64,2,1536]{3,1,2,0:T(8,128)S(1)} %fusion.1), channel_id=1, replica_groups=mesh['groups'=2,'ep'=32,'tp'=4,'dp'=2] {'tp'}, dimensions={0} | all-to-all | bytes 6291456 | tf_op jit(solution)/shard_map/all_to_all | solution.py:36
  173.7 2.2 reduce_sum.42
  175.9 1.1 copy.31
  177.0 7.5 %all-to-all-start.3 = ((bf16[64,2,1536]{2,1,0:T(2,128)(2,1)}), bf16[64,2,1536]{2,1,0:T(2,128)(2,1)S(1)}, u32[]{:S(2)}, u32[]{:S(2)}) async-start(bf16[64,2,1536]{2,1,0:T(2,128)(2,1)} %copy.31), calls=%async_computation.3 | async-start | bytes 786432 | tf_op jit(solution)/shard_map/all_to_all | solution.py:80
  184.8 85.2 %psum.21 = f32[64]{0:T(128)S(1)} all-reduce(f32[64]{0:T(128)S(1)} %convert_element_type.31), channel_id=1, replica_groups=mesh['groups'=2,'ep'=32,'tp'=4,'dp'=2] {'ep'}, use_global_device_ids=true, to_apply=%region_6.7 | all-reduce | flops 64 | bytes 512 | tf_op jit(solution)/shard_map/psum | solution.py:9
  270.0 8.9 %psum.22 = f32[64]{0:T(128)S(1)} all-reduce(f32[64]{0:T(128)S(1)} %psum.21), channel_id=1, replica_groups=mesh['groups'=2,'ep'=32,'tp'=4,'dp'=2] {'tp'}, use_global_device_ids=true, to_apply=%region_7.8 | all-reduce | flops 64 | bytes 512 | tf_op jit(solution)/shard_map/psum | solution.py:9
  278.9 2.5 psum.23
  281.4 0.5 convert_element_type.32
  282.0 0.1 reshape.66
  282.1 0.7 gather_fusion
  282.9 1.1 multiply_reduce_fusion
  (22 shorter events, 0.7 us)
Async XLA Ops:
  0.6 133.3 %copy-start = (bf16[1,1536,384]{2,1,0:T(8,128)(2,1)S(1)}, bf16[1,1536,384]{2,1,0:T(8,128)(2,1)}, u32[]{:S(2)}) copy-start(bf16[1,1536,384]{2,1,0:T(8,128)(2,1)} %param.11) | copy-start | bytes 3538948
  129.9 2.9 %copy-start.1 = (bf16[512,1536]{1,0:T(8,128)(2,1)S(1)}, bf16[512,1536]{1,0:T(8,128)(2,1)}, u32[]{:S(2)}) copy-start(bf16[512,1536]{1,0:T(8,128)(2,1)} %reshape_reshape.4) | copy-start | bytes 4718596
  129.9 2.9 %copy-start.3 = (bf16[1,1536,384]{2,1,0:T(8,128)(2,1)S(1)}, bf16[1,1536,384]{2,1,0:T(8,128)(2,1)}, u32[]{:S(2)}) copy-start(bf16[1,1536,384]{2,1,0:T(8,128)(2,1)} %param.10) | copy-start | bytes 3538948
  175.9 8.8 %copy-start.2 = (f32[16,4]{0,1:T(4,128)S(1)}, f32[16,4]{0,1:T(4,128)}, u32[]{:S(2)}) copy-start(f32[16,4]{0,1:T(4,128)} %param.8) | copy-start | bytes 772
  177.0 104.9 %all-to-all-start.3 = ((bf16[64,2,1536]{2,1,0:T(2,128)(2,1)}), bf16[64,2,1536]{2,1,0:T(2,128)(2,1)S(1)}, u32[]{:S(2)}, u32[]{:S(2)}) async-start(bf16[64,2,1536]{2,1,0:T(2,128)(2,1)} %copy.31), calls=%async_computation.3 | async-start | bytes 786432 | tf_op jit(solution)/shard_map/all_to_all | solution.py:80
where the time goes:
time: 286 us; the launch traced here: 284 us
  blocking collectives  259 us (91%)
  starting transfers between devices  7.55 us (3%)
  matrix products  5.98 us (2%)
  local copies, waits for them, and re-layouts  5.97 us (2%)
  other arithmetic  4.29 us (2%)
    all_to_all x1, blocking collectives, per_device(): lax.all_to_all(outgoing, ('ep', 'dp'), split_axis=0, concat_axis=0, tiled...  100 us
    psum x3, blocking collectives, one_axis_at_a_time(): array = lax.psum(array, axis)  96.6 us
    all_to_all x1, blocking collectives, sent_and_summed(): lax.all_to_all(blocks, axis, split_axis=0, concat_axis=0, tiled=True)  38.7 us
    all_to_all x1, blocking collectives, copy_for_each(): return lax.all_to_all(copies, axis, split_axis=0, concat_axis=0, tiled=True)  24 us
    all_to_all x1, starting transfers between devices, per_device(): lax.all_to_all(finished, ('ep', 'dp'), split_axis=0, concat_axis=0, tiled...  7.55 us
  transfers between devices with their start and end apart: 1, of which 0 were waited for; matrix products, arithmetic and copies ran while one was open for 0% of the time, Pallas kernels for 0%

commit v1 on v0

v1 whole, which is shorter than its diff:
```python
import functools

import jax
import jax.numpy as jnp
from jax import lax
from jax.experimental import pallas as pl
from jax.experimental.pallas import tpu as pltpu
from jax.sharding import PartitionSpec as P

MESH = pl.DeviceIdType.MESH
BF16 = jnp.bfloat16
F32 = jnp.float32
LANES = 128
CAP = 2
GROUPS = ((0, 1), (1, 2), (3, 1))


def iota(shape, dim):
    return lax.broadcasted_iota(jnp.int32, shape, dim)


def dot(a, b):
    return jnp.dot(a, b, preferred_element_type=F32)


def dot_nt(a, b):
    return lax.dot_general(a, b, (((1,), (1,)), ((), ())), preferred_element_type=F32)


def kernel(
    ring, tokens, ids, gates, wg_hbm, wu_hbm, wd_hbm, out, loads,
    wg, wu, wd, chunk, packed, xrecv, xf, yf, yb, ra, rb, sa, sb, eo, ret,
    gsel, oparts, ksend, krecv, fsend, frecv, cnt, crecv, csum, cx,
    wsem, cs, cr, c3s, c3r, ls, lr, x1s, x1r, x2s, x2r, r1s, r1r, r2s, r2r,
    ts, tr, k3s, k3r, kfs, kfr, ns, nr, ncs, ncr,
):
    jump = ring // 4
    half = jump // 2
    slots = 2 * jump
    tok, width = tokens.shape
    qw = width // 4
    tiles = qw // LANES
    piece = 4 * CAP
    prow = slots * piece
    lanes = chunk.shape[2] - width
    meta = lanes // 2
    experts = meta // CAP
    top = ids.shape[1]
    cols = (0, qw, 2 * qw + meta, 3 * qw + meta)
    mid = 2 * qw + meta

    z, x, c = lax.axis_index("ep"), lax.axis_index("tp"), lax.axis_index("dp")
    own = (half - c) * 2 + c

    def at_z(d):
        return {"ep": lax.rem(z + d + 2 * ring, ring), "tp": x, "dp": c}

    def at_x(d):
        return {"ep": z, "tp": lax.rem(x + d + 4, 4), "dp": c}

    def out_peer(s):
        return {"ep": lax.rem(z + s // 2 - half + c + ring, ring), "tp": x, "dp": lax.rem(s, 2)}

    def in_peer(s):
        core = lax.rem(s, 2)
        return {"ep": lax.rem(z - s // 2 + half - core + ring, ring), "tp": x, "dp": core}

    def remote(src, dst, send, recv, peer):
        return pltpu.make_async_remote_copy(
            src_ref=src, dst_ref=dst, send_sem=send, recv_sem=recv, device_id=peer, device_id_type=MESH
        )

    def arrived(ref, sem):
        pltpu.make_async_copy(ref, ref, sem).wait()

    weights = [
        pltpu.make_async_copy(src, dst, wsem.at[i])
        for i, (src, dst) in enumerate(((wg_hbm, wg), (wu_hbm, wu), (wd_hbm, wd)))
    ]

    barrier = pltpu.get_barrier_semaphore()

    def greet(peer):
        pl.semaphore_signal(barrier, inc=1, device_id=peer, device_id_type=MESH)

    greet(at_z(jump))
    greet(at_z(-jump))

    def greet_local(i, carry):
        s = lax.rem(own + i, slots)
        greet(out_peer(s))
        greet(in_peer(s))
        return carry

    lax.fori_loop(1, slots, greet_local, 0)
    greet(at_x(1))
    greet(at_x(-1))
    for copy in weights:
        copy.start()

    lane = iota((tok, meta), 1)
    expert_lane = jnp.where(lane >= experts, lane - experts, lane)
    rank_lane = jnp.where(lane >= experts, 1, 0)
    hit = jnp.zeros((tok, meta), F32)
    gate = jnp.zeros((tok, meta), F32)
    for k in range(top):
        same = ids[:, k : k + 1] == expert_lane
        hit = hit + jnp.where(same, 1.0, 0.0)
        gate = gate + jnp.where(same, gates[:, k : k + 1], 0.0)
    earlier = jnp.where(iota((tok, tok), 1) < iota((tok, tok), 0), 1.0, 0.0).astype(BF16)
    rank = dot(earlier, hit.astype(BF16))
    gate = jnp.where(rank == rank_lane.astype(F32), gate, 0.0)
    gate_hi = gate.astype(BF16)
    gate_lo = (gate - gate_hi.astype(F32)).astype(BF16)
    chunk[0, :, 0 : 2 * qw] = tokens[:, 0 : 2 * qw]
    chunk[0, :, 2 * qw : mid] = gate_hi
    chunk[0, :, mid : mid + 2 * qw] = tokens[:, 2 * qw :]
    chunk[0, :, mid + 2 * qw :] = gate_lo

    pl.semaphore_wait(barrier, 2 * (slots - 1) + 4)

    jumps = [
        remote(chunk.at[0], chunk.at[1], cs.at[0], cr.at[0], at_z(jump)),
        remote(chunk.at[0], chunk.at[2], cs.at[1], cr.at[1], at_z(-jump)),
    ]
    for copy in jumps:
        copy.start()

    row = iota((prow, meta), 0)
    lane = iota((prow, meta), 1)
    row_slot = row // piece
    row_z = lax.rem(z + row_slot // 2 - half + c + ring, ring)
    row_expert = row_z * 2 + lax.rem(row_slot, 2)
    row_rank = lax.rem(row // 4, CAP)
    pick = jnp.where(row_rank * experts + row_expert == lane, 1.0, 0.0).astype(BF16)
    quarter_r = lax.rem(iota((prow, 4 * tok), 0), 4) == iota((prow, 4 * tok), 1) // tok
    quarter_c = lax.rem(iota((4 * tok, prow), 1), 4) == iota((4 * tok, prow), 0) // tok

    def pack(m):
        hi = chunk[m, :, 2 * qw : mid]
        lo = chunk[m, :, mid + 2 * qw :]
        used = jnp.where(hi.astype(F32) > 0.0, 1.0, 0.0)
        count = jnp.sum(used, axis=0, keepdims=True)
        used = used.astype(BF16)
        select = dot_nt(pick, jnp.concatenate([used] * 4, axis=0))
        select = jnp.where(quarter_r, select, 0.0).astype(BF16)
        quarters = jnp.concatenate([chunk[m, :, o : o + qw] for o in cols], axis=0)
        rows = dot(select, quarters).astype(BF16)
        packed[pl.ds(m * slots, slots)] = rows.reshape(slots, piece, qw)
        for h, part in enumerate((hi, lo)):
            mix = dot_nt(jnp.concatenate([part] * 4, axis=0), pick)
            gsel[m, pl.ds(h * 4 * tok, 4 * tok), :] = jnp.where(quarter_c, mix, 0.0).astype(BF16)
        return count

    def send_local(m):
        def body(i, carry):
            s = lax.rem(own + i, slots)
            remote(
                packed.at[m * slots + s],
                xrecv.at[0, m * slots + lax.rem(s // 2 * 2 + c, slots)],
                ls.at[m], lr.at[m], out_peer(s),
            ).start()
            return carry

        pltpu.make_async_copy(packed.at[m * slots + own], xrecv.at[0, m * slots + own], lr.at[m]).start()
        lax.fori_loop(1, slots, body, 0)

    def span(g):
        m0, nm = GROUPS[g]
        return m0 * slots, nm * slots

    def halves(g):
        s0, n = span(g)
        return pl.ds(s0, n // 2), pl.ds(s0 + n // 2, n // 2)

    def x1_copies(g):
        s0, n = span(g)
        part = xrecv.at[0, pl.ds(s0, n)]
        return [
            remote(part, xrecv.at[1, pl.ds(s0, n)], x1s.at[g, 0], x1r.at[g, 0], at_x(1)),
            remote(part, xrecv.at[3, pl.ds(s0, n)], x1s.at[g, 1], x1r.at[g, 1], at_x(-1)),
        ]

    def x2_copies(g):
        a, b = halves(g)
        return [
            remote(xrecv.at[1, a], xrecv.at[2, a], x2s.at[g, 0], x2r.at[g, 0], at_x(1)),
            remote(xrecv.at[3, b], xrecv.at[2, b], x2s.at[g, 1], x2r.at[g, 1], at_x(-1)),
        ]

    def gather_1(g):
        m0, nm = GROUPS[g]
        for m in range(m0, m0 + nm):
            arrived(xrecv.at[0, pl.ds(m * slots, slots)], lr.at[m])
        for copy in x1_copies(g):
            copy.start()

    def gather_2(g):
        for one, two in zip(x1_copies(g), x2_copies(g)):
            one.wait_recv()
            two.start()

    def ffn(g):
        s0, n = span(g)
        count = 4 * n * piece
        rows = count // 4
        for copy in x2_copies(g):
            copy.wait_recv()
        for j in range(tiles):
            arrivals = xrecv[:, pl.ds(s0, n), :, j * LANES : (j + 1) * LANES]
            xf[j, pl.ds(0, count)] = arrivals.astype(F32).reshape(count, LANES)
        full = jnp.concatenate(
            [
                xf[j, pl.ds(q, rows, stride=4), :].astype(BF16)
                for q in range(4)
                for j in range(tiles)
            ],
            axis=1,
        )
        gate_value = dot(full, wg[...])
        up_value = dot(full, wu[...])
        hidden = (gate_value / (1.0 + jnp.exp(-gate_value)) * up_value).astype(BF16)
        for q in range(4):
            terms = dot_nt(hidden, wd[pl.ds(q * qw, qw), :])
            for j in range(tiles):
                place = pl.ds(4 * s0 * piece + q, rows, stride=4)
                yf[j, place, :] = terms[:, j * LANES : (j + 1) * LANES]
        yb[1, pl.ds(s0, n)] = partial(g, 2, 0, n).astype(BF16)
        for copy in r1_copies(g):
            copy.start()

    def partial(g, column, first, number):
        s0, n = span(g)
        start = (4 * s0 + column * n + first) * piece
        parts = [yf[j, pl.ds(start, number * piece), :] for j in range(tiles)]
        return jnp.concatenate(parts, axis=1).reshape(number, piece, qw)

    def r1_copies(g):
        a, b = halves(g)
        return [
            remote(yb.at[1, a], ra.at[a], r1s.at[g, 0], r1r.at[g, 0], at_x(1)),
            remote(yb.at[1, b], rb.at[b], r1s.at[g, 1], r1r.at[g, 1], at_x(-1)),
        ]

    def r2_copies(g):
        s0, n = span(g)
        part = pl.ds(s0, n)
        return [
            remote(yb.at[2, part], sa.at[part], r2s.at[g, 0], r2r.at[g, 0], at_x(1)),
            remote(yb.at[0, part], sb.at[part], r2s.at[g, 1], r2r.at[g, 1], at_x(-1)),
        ]

    def reduce_1(g):
        s0, n = span(g)
        a, b = halves(g)
        one, two = r1_copies(g), r2_copies(g)
        yb[2, b] = partial(g, 3, n // 2, n // 2).astype(BF16)
        yb[0, a] = partial(g, 1, 0, n // 2).astype(BF16)
        one[0].wait_recv()
        yb[2, a] = (partial(g, 3, 0, n // 2) + ra[a].astype(F32)).astype(BF16)
        two[0].start()
        one[1].wait_recv()
        yb[0, b] = (partial(g, 1, n // 2, n // 2) + rb[b].astype(F32)).astype(BF16)
        two[1].start()

    def reduce_2(g):
        m0, nm = GROUPS[g]
        s0, n = span(g)
        part = pl.ds(s0, n)
        for copy in r2_copies(g):
            copy.wait_recv()
        eo[part] = (partial(g, 0, 0, n) + sa[part].astype(F32) + sb[part].astype(F32)).astype(BF16)
        for m in range(m0, m0 + nm):
            send_back(m)

    def send_back(m):
        def body(i, carry):
            s = lax.rem(own + i, slots)
            remote(
                eo.at[m * slots + s],
                ret.at[m * slots + lax.rem(s // 2 * 2 + c, slots)],
                ts.at[m], tr.at[m], in_peer(s),
            ).start()
            return carry

        pltpu.make_async_copy(eo.at[m * slots + own], ret.at[m * slots + own], tr.at[m]).start()
        lax.fori_loop(1, slots, body, 0)

    def combine(m):
        part = pl.ds(m * slots, slots)
        arrived(ret.at[part], tr.at[m])
        rows = ret[part].astype(F32).reshape(prow, qw).astype(BF16)
        both = dot(gsel[m], rows)
        quarters = both[0 : 4 * tok] + both[4 * tok :]
        return jnp.concatenate([quarters[q * tok : (q + 1) * tok] for q in range(4)], axis=1)

    def k3_copies():
        low, high = pl.ds(0, 2 * qw), pl.ds(2 * qw, 2 * qw)
        return [
            remote(ksend.at[:, low], krecv.at[:, low], k3s.at[0], k3r.at[0], at_z(-jump)),
            remote(ksend.at[:, high], krecv.at[:, high], k3s.at[1], k3r.at[1], at_z(jump)),
        ]

    def kf_copies():
        return [
            remote(fsend.at[0], frecv.at[0], kfs.at[0], kfr.at[0], at_z(-jump)),
            remote(fsend.at[1], frecv.at[1], kfs.at[1], kfr.at[1], at_z(jump)),
        ]

    count = pack(0)
    send_local(0)
    low, high = pl.ds(0, mid), pl.ds(mid, mid)
    onward = [
        remote(chunk.at[1, :, low], chunk.at[3, :, low], c3s.at[0], c3r.at[0], at_z(jump)),
        remote(chunk.at[2, :, high], chunk.at[3, :, high], c3s.at[1], c3r.at[1], at_z(-jump)),
    ]
    for first, second in zip(jumps, onward):
        first.wait_recv()
        second.start()
    count = count + pack(1)
    send_local(1)
    count = count + pack(2)
    send_local(2)
    gather_1(0)
    gather_2(0)
    gather_1(1)
    for copy in onward:
        copy.wait_recv()
    count = count + pack(3)
    send_local(3)

    cnt[...] = count

    def send_count(i, carry):
        s = lax.rem(own + i, slots)
        remote(cnt, crecv.at[lax.rem(s // 2 * 2 + c, slots)], ns, nr, out_peer(s)).start()
        return carry

    pltpu.make_async_copy(cnt, crecv.at[own], nr).start()
    lax.fori_loop(1, slots, send_count, 0)

    gather_2(1)
    for copy in weights:
        copy.wait()
    ffn(0)
    gather_1(2)
    ffn(1)
    gather_2(2)
    reduce_1(0)
    reduce_1(1)
    reduce_2(0)
    ffn(2)
    reduce_2(1)

    arrived(crecv, nr)
    csum[...] = jnp.sum(crecv[...], axis=0)
    count_1 = [
        remote(csum, cx.at[0], ncs.at[0], ncr.at[0], at_x(1)),
        remote(csum, cx.at[1], ncs.at[1], ncr.at[1], at_x(-1)),
    ]
    count_2 = remote(cx.at[0], cx.at[2], ncs.at[2], ncr.at[2], at_x(1))
    for copy in count_1:
        copy.start()

    reduce_1(2)
    count_1[0].wait_recv()
    count_2.start()
    oparts[...] = combine(0)
    reduce_2(2)
    near = [combine(1), combine(2)]
    count_1[1].wait_recv()
    count_2.wait_recv()
    total = csum[...] + cx[0] + cx[1] + cx[2]
    total = total[:, 0:experts] + total[:, experts:]
    loads[...] = total.astype(jnp.int32)

    ksend[...] = combine(3).astype(BF16)
    for copy in k3_copies():
        copy.start()
    first, second = k3_copies()
    last = kf_copies()
    first.wait_recv()
    fsend[0, :, 0 : 2 * qw] = (near[0][:, 0 : 2 * qw] + krecv[:, 0 : 2 * qw].astype(F32)).astype(BF16)
    fsend[0, :, 2 * qw :] = near[0][:, 2 * qw :].astype(BF16)
    last[0].start()
    second.wait_recv()
    fsend[1, :, 2 * qw :] = (near[1][:, 2 * qw :] + krecv[:, 2 * qw :].astype(F32)).astype(BF16)
    fsend[1, :, 0 : 2 * qw] = near[1][:, 0 : 2 * qw].astype(BF16)
    last[1].start()
    for copy in last:
        copy.wait_recv()
    out[...] = (oparts[...] + frecv[0].astype(F32) + frecv[1].astype(F32)).astype(BF16)

    sends = jumps + onward + k3_copies() + last + count_1 + [count_2]
    for g in range(len(GROUPS)):
        sends += x1_copies(g) + x2_copies(g) + r1_copies(g) + r2_copies(g)
    for copy in sends:
        copy.wait_send()
    for m in range(4):
        arrived(packed.at[pl.ds(m * slots, slots - 1)], ls.at[m])
        arrived(eo.at[pl.ds(m * slots, slots - 1)], ts.at[m])
    arrived(crecv.at[pl.ds(0, slots - 1)], ns)


def per_device(tokens, expert_ids, gate_weights, w_gate, w_up, w_down):
    tok, width = tokens.shape
    hidden = w_gate.shape[2]
    ring = lax.axis_size("ep")
    experts = ring * lax.axis_size("dp")
    slots = 2 * (ring // 4)
    qw = width // 4
    piece = 4 * CAP
    meta = CAP * experts
    prow = slots * piece
    ng = len(GROUPS)
    vmem = pltpu.VMEM
    dma = pltpu.SemaphoreType.DMA
    block = (4 * slots, piece, qw)
    scratch = [
        vmem((width, hidden), BF16), vmem((width, hidden), BF16), vmem((width, hidden), BF16),
        vmem((4, tok, width + 2 * meta), BF16),
        vmem(block, BF16),
        vmem((4, *block), BF16),
        vmem((qw // LANES, 2 * 4 * prow, LANES), F32),
        vmem((qw // LANES, 4 * 4 * prow, LANES), F32),
        vmem((3, *block), BF16),
        vmem(block, BF16), vmem(block, BF16), vmem(block, BF16), vmem(block, BF16),
        vmem(block, BF16), vmem(block, BF16),
        vmem((4, 8 * tok, prow), BF16),
        vmem((tok, width), F32),
        vmem((tok, width), BF16), vmem((tok, width), BF16),
        vmem((2, tok, width), BF16), vmem((2, tok, width), BF16),
        vmem((1, meta), F32), vmem((slots, 1, meta), F32),
        vmem((1, meta), F32), vmem((3, 1, meta), F32),
        dma((3,)), dma((2,)), dma((2,)), dma((2,)), dma((2,)),
        dma((4,)), dma((4,)),
        dma((ng, 2)), dma((ng, 2)), dma((ng, 2)), dma((ng, 2)),
        dma((ng, 2)), dma((ng, 2)), dma((ng, 2)), dma((ng, 2)),
        dma((4,)), dma((4,)), dma((2,)), dma((2,)), dma((2,)), dma((2,)),
        dma(()), dma(()), dma((3,)), dma((3,)),
    ]
    in_vmem = pl.BlockSpec(memory_space=pltpu.VMEM)
    in_any = pl.BlockSpec(memory_space=pl.ANY)
    mixed, loads = pl.pallas_call(
        functools.partial(kernel, ring),
        out_shape=(
            jax.ShapeDtypeStruct((tok, width), BF16),
            jax.ShapeDtypeStruct((1, experts), jnp.int32),
        ),
        in_specs=[in_vmem, in_vmem, in_vmem, in_any, in_any, in_any],
        out_specs=(in_vmem, in_vmem),
        scratch_shapes=scratch,
        compiler_params=pltpu.CompilerParams(
            collective_id=0, has_side_effects=True, vmem_limit_bytes=60 * 1024 * 1024
        ),
        name="routed_ffn",
    )(tokens, expert_ids, gate_weights, w_gate[0], w_up[0], w_down[0])
    return mixed, loads[0]


def solution(mesh):
    return jax.shard_map(
        per_device,
        mesh=mesh,
        in_specs=(
            P(("groups", "ep", "tp", "dp"), None),
            P(("groups", "ep", "tp", "dp"), None),
            P(("groups", "ep", "tp", "dp"), None),
            P(("ep", "dp"), None, "tp"),
            P(("ep", "dp"), None, "tp"),
            P(("ep", "dp"), None, "tp"),
        ),
        out_specs=(P(("groups", "ep", "tp", "dp"), None), P("groups")),
        check_vma=False,
    )
```

time: 286 us -> 140 us (0.49)
  blocking collectives: 259 us -> 0 us
  Pallas kernels: 0 us -> 133 us
  starting transfers between devices: 7.55 us -> 0 us
  matrix products: 5.98 us -> 0 us
  other arithmetic: 4.29 us -> 0 us
    all_to_all x3 -> x0, blocking collectives: 163 us -> none  [the longest x1 100 us: per_device(): lax.all_to_all(outgoing, ('ep', 'dp'), split_axis=0, concat_axis=0, tiled...]
    pallas_call x0 -> x1, Pallas kernels: none -> 133 us  [per_device(): pl.pallas_call(functools.partial(kernel, ring), out_shape=(jax.ShapeDtype...]
    psum x3 -> x0, blocking collectives: 96.6 us -> none  [one_axis_at_a_time(): array = lax.psum(array, axis)]
    all_to_all x1 -> x0, starting transfers between devices: 7.55 us -> none  [per_device(): lax.all_to_all(finished, ('ep', 'dp'), split_axis=0, concat_axis=0, tiled...]
    dot_general x4 -> x0, matrix products: 5.98 us -> none  [the longest x1 2.86 us: expert_apply(): jnp.dot(token_rows, gate_part, preferred_element_type=jnp.float32)]
    unnamed x10 -> x4, local copies, waits for them, and re-layouts: 0.96 us -> 5.25 us
    reduce_sum x3 -> x0, other arithmetic: 3.47 us -> none  [the longest x1 2.2 us: sent_and_summed(): return arrived.sum(axis=0)]
  transfers between devices with their start and end apart: 1 -> 0, of which waited for: 0 -> 0; matrix products, arithmetic and copies ran while one was open for 0% -> 0% of each run, Pallas kernels for 0% -> 0%
where the time goes in v1:
time: 140 us; the launch traced here: 139 us
  Pallas kernels  133 us (95%)
  local copies, waits for them, and re-layouts  5.25 us (4%)
    pallas_call x1, Pallas kernels, per_device(): pl.pallas_call(functools.partial(kernel, ring), out_shape=(jax.ShapeDtype...  133 us
    unnamed x4, local copies, waits for them, and re-layouts  5.25 us

profile of v1, /device:TPU:40, one launch (start us, length us, event | category | flops | bytes accessed | tf_op | source)
XLA Modules:
  0.0 139.2 jit_solution(1451129968348166551)
XLA Ops:
  0.6 1.4 copy.8.ids
  2.0 1.3 copy.9.gates
  3.3 133.4 %routed_ffn.1 = (bf16[16,1536]{1,0:T(8,128)(2,1)}, s32[1,64]{1,0:T(1,128)}) custom-call(bf16[16,1536]{1,0:T(8,128)(2,1)} %tokens.1, s32[16,4]{1,0:T(8,128)} %copy.8.ids, f32[16,4]{1,0:T(8,128)} %copy.9.gates, bf16[1536,384]{1,0:T(8,128)(2,1)} %bitcast.4, bf16[1536,384]{1,0:T(8,128)(2,1)} %bitcast.5, bf16[1536,384]{1,0:T(8,128)(2,1)} %bitcast.6), custom_call_target="tpu_custom_call" | custom-call | tf_op jit(solution)/shard_map/routed_ffn/pallas_call | solution.py:444
  136.7 1.4 %copy.12 = bf16[16,1536]{1,0:T(8,128)(2,1)} copy(bf16[16,1536]{1,0:T(8,128)(2,1)} %get-tuple-element.8) | data formatting | bytes 98304
  138.1 1.1 copy.13

commit v2 on v1

--- a/solution.py
+++ b/solution.py
@@ -12,7 +12,9 @@
 F32 = jnp.float32
 LANES = 128
 CAP = 2
-GROUPS = ((0, 1), (1, 2), (3, 1))
+N0, S0, N12, N3, S12, S3 = range(6)
+GROUPS = ((1, 0, 1), (0, 0, 1), (1, 1, 2), (1, 3, 1), (0, 1, 2), (0, 3, 1))
+DIRECT = (N0, S0, N3, S3)
 
 
 def iota(shape, dim):
@@ -28,10 +30,10 @@
 
 
 def kernel(
-    ring, tokens, ids, gates, wg_hbm, wu_hbm, wd_hbm, out, loads,
-    wg, wu, wd, chunk, packed, xrecv, xf, yf, yb, ra, rb, sa, sb, eo, ret,
+    ring, tokens_hbm, ids_hbm, gates_hbm, wg_hbm, wu_hbm, wd_hbm, out, loads,
+    tokens, ids, gates, wg, wu, wd, chunk, packed, xrecv, xf, yf, yb, ra, rb, sa, sb, eo, ret,
     gsel, oparts, ksend, krecv, fsend, frecv, cnt, crecv, csum, cx,
-    wsem, cs, cr, c3s, c3r, ls, lr, x1s, x1r, x2s, x2r, r1s, r1r, r2s, r2r,
+    wsem, isem, cs, cr, ls, lr, x1s, x1r, x2s, x2r, r1s, r1r, r2s, r2r,
     ts, tr, k3s, k3r, kfs, kfr, ns, nr, ncs, ncr,
 ):
     jump = ring // 4
@@ -45,7 +47,7 @@
     lanes = chunk.shape[2] - width
     meta = lanes // 2
     experts = meta // CAP
-    top = ids.shape[1]
+    top = ids.shape[0]
     cols = (0, qw, 2 * qw + meta, 3 * qw + meta)
     mid = 2 * qw + meta
 
@@ -77,6 +79,13 @@
         pltpu.make_async_copy(src, dst, wsem.at[i])
         for i, (src, dst) in enumerate(((wg_hbm, wg), (wu_hbm, wu), (wd_hbm, wd)))
     ]
+
+    inputs = [
+        pltpu.make_async_copy(src, dst, isem.at[i])
+        for i, (src, dst) in enumerate(((ids_hbm, ids), (gates_hbm, gates), (tokens_hbm, tokens)))
+    ]
+    for copy in inputs:
+        copy.start()
 
     barrier = pltpu.get_barrier_semaphore()
 
@@ -95,34 +104,51 @@
     lax.fori_loop(1, slots, greet_local, 0)
     greet(at_x(1))
     greet(at_x(-1))
+    greet(at_x(2))
     for copy in weights:
         copy.start()
 
-    lane = iota((tok, meta), 1)
-    expert_lane = jnp.where(lane >= experts, lane - experts, lane)
-    rank_lane = jnp.where(lane >= experts, 1, 0)
-    hit = jnp.zeros((tok, meta), F32)
-    gate = jnp.zeros((tok, meta), F32)
+    for copy in inputs:
+        copy.wait()
+
+    line = iota((meta, tok), 0)
+    line_expert = jnp.where(line >= experts, line - experts, line)
+    line_rank = jnp.where(line >= experts, 1.0, 0.0)
+    hit = jnp.zeros((meta, tok), F32)
+    gate = jnp.zeros((meta, tok), F32)
     for k in range(top):
-        same = ids[:, k : k + 1] == expert_lane
+        same = ids[k : k + 1, :] == line_expert
         hit = hit + jnp.where(same, 1.0, 0.0)
-        gate = gate + jnp.where(same, gates[:, k : k + 1], 0.0)
-    earlier = jnp.where(iota((tok, tok), 1) < iota((tok, tok), 0), 1.0, 0.0).astype(BF16)
-    rank = dot(earlier, hit.astype(BF16))
-    gate = jnp.where(rank == rank_lane.astype(F32), gate, 0.0)
+        gate = gate + jnp.where(same, gates[k : k + 1, :], 0.0)
+    row, column = iota((tok, tok), 0), iota((tok, tok), 1)
+    rank = dot(hit.astype(BF16), jnp.where(row < column, 1.0, 0.0).astype(BF16))
+    gate = jnp.where(rank == line_rank, gate, 0.0)
     gate_hi = gate.astype(BF16)
     gate_lo = (gate - gate_hi.astype(F32)).astype(BF16)
+    unit = jnp.where(row == column, 1.0, 0.0).astype(BF16)
+    gate_hi = dot_nt(unit, gate_hi).astype(BF16)
+    gate_lo = dot_nt(unit, gate_lo).astype(BF16)
     chunk[0, :, 0 : 2 * qw] = tokens[:, 0 : 2 * qw]
     chunk[0, :, 2 * qw : mid] = gate_hi
     chunk[0, :, mid : mid + 2 * qw] = tokens[:, 2 * qw :]
     chunk[0, :, mid + 2 * qw :] = gate_lo
 
-    pl.semaphore_wait(barrier, 2 * (slots - 1) + 4)
+    pl.semaphore_wait(barrier, 2 * (slots - 1) + 5)
+
+    low, high = pl.ds(0, mid), pl.ds(mid, mid)
+
+    def jump_copy(i, part, source, target, where):
+        return remote(
+            chunk.at[source, :, part], chunk.at[target, :, part], cs.at[i], cr.at[i], at_z(where)
+        )
 
     jumps = [
-        remote(chunk.at[0], chunk.at[1], cs.at[0], cr.at[0], at_z(jump)),
-        remote(chunk.at[0], chunk.at[2], cs.at[1], cr.at[1], at_z(-jump)),
+        jump_copy(0, low, 0, 1, jump),
+        jump_copy(1, high, 0, 2, -jump),
+        jump_copy(2, high, 0, 1, jump),
+        jump_copy(3, low, 0, 2, -jump),
     ]
+    onward = [jump_copy(4, low, 1, 3, jump), jump_copy(5, high, 2, 3, -jump)]
     for copy in jumps:
         copy.start()
 
@@ -157,17 +183,18 @@
             s = lax.rem(own + i, slots)
             remote(
                 packed.at[m * slots + s],
-                xrecv.at[0, m * slots + lax.rem(s // 2 * 2 + c, slots)],
-                ls.at[m], lr.at[m], out_peer(s),
+                xrecv.at[0, (c * 4 + m) * jump + s // 2],
+                ls.at[m], lr.at[c * 4 + m], out_peer(s),
             ).start()
             return carry
 
-        pltpu.make_async_copy(packed.at[m * slots + own], xrecv.at[0, m * slots + own], lr.at[m]).start()
+        here = xrecv.at[0, (c * 4 + m) * jump + own // 2]
+        pltpu.make_async_copy(packed.at[m * slots + own], here, lr.at[c * 4 + m]).start()
         lax.fori_loop(1, slots, body, 0)
 
     def span(g):
-        m0, nm = GROUPS[g]
-        return m0 * slots, nm * slots
+        core, m0, nm = GROUPS[g]
+        return (core * 4 + m0) * jump, nm * jump
 
     def halves(g):
         s0, n = span(g)
@@ -176,7 +203,11 @@
     def x1_copies(g):
         s0, n = span(g)
         part = xrecv.at[0, pl.ds(s0, n)]
-        return [
+        if g in DIRECT:
+            across = [remote(part, xrecv.at[2, pl.ds(s0, n)], x2s.at[g, 0], x2r.at[g, 0], at_x(2))]
+        else:
+            across = []
+        return across + [
             remote(part, xrecv.at[1, pl.ds(s0, n)], x1s.at[g, 0], x1r.at[g, 0], at_x(1)),
             remote(part, xrecv.at[3, pl.ds(s0, n)], x1s.at[g, 1], x1r.at[g, 1], at_x(-1)),
         ]
@@ -189,9 +220,9 @@
         ]
 
     def gather_1(g):
-        m0, nm = GROUPS[g]
-        for m in range(m0, m0 + nm):
-            arrived(xrecv.at[0, pl.ds(m * slots, slots)], lr.at[m])
+        core, m0, nm = GROUPS[g]
+        for n in range(core * 4 + m0, core * 4 + m0 + nm):
+            arrived(xrecv.at[0, pl.ds(n * jump, jump)], lr.at[n])
         for copy in x1_copies(g):
             copy.start()
 
@@ -204,7 +235,7 @@
         s0, n = span(g)
         count = 4 * n * piece
         rows = count // 4
-        for copy in x2_copies(g):
+        for copy in x1_copies(g) if g in DIRECT else x2_copies(g):
             copy.wait_recv()
         for j in range(tiles):
             arrivals = xrecv[:, pl.ds(s0, n), :, j * LANES : (j + 1) * LANES]
@@ -225,9 +256,15 @@
             for j in range(tiles):
                 place = pl.ds(4 * s0 * piece + q, rows, stride=4)
                 yf[j, place, :] = terms[:, j * LANES : (j + 1) * LANES]
-        yb[1, pl.ds(s0, n)] = partial(g, 2, 0, n).astype(BF16)
+        part = pl.ds(s0, n)
+        yb[1, part] = partial(g, 2, 0, n).astype(BF16)
         for copy in r1_copies(g):
             copy.start()
+        if g in DIRECT:
+            yb[2, part] = partial(g, 3, 0, n).astype(BF16)
+            yb[0, part] = partial(g, 1, 0, n).astype(BF16)
+            for copy in r2_copies(g):
+                copy.start()
 
     def partial(g, column, first, number):
         s0, n = span(g)
@@ -237,6 +274,10 @@
 
     def r1_copies(g):
         a, b = halves(g)
+        if g in DIRECT:
+            s0, n = span(g)
+            part = pl.ds(s0, n)
+            return [remote(yb.at[1, part], ra.at[part], r1s.at[g, 0], r1r.at[g, 0], at_x(2))]
         return [
             remote(yb.at[1, a], ra.at[a], r1s.at[g, 0], r1r.at[g, 0], at_x(1)),
             remote(yb.at[1, b], rb.at[b], r1s.at[g, 1], r1r.at[g, 1], at_x(-1)),
@@ -264,27 +305,44 @@
         two[1].start()
 
     def reduce_2(g):
-        m0, nm = GROUPS[g]
+        core, m0, nm = GROUPS[g]
         s0, n = span(g)
         part = pl.ds(s0, n)
         for copy in r2_copies(g):
             copy.wait_recv()
-        eo[part] = (partial(g, 0, 0, n) + sa[part].astype(F32) + sb[part].astype(F32)).astype(BF16)
+        total = partial(g, 0, 0, n) + sa[part].astype(F32) + sb[part].astype(F32)
+        if g in DIRECT:
+            for copy in r1_copies(g):
+                copy.wait_recv()
+            total = total + ra[part].astype(F32)
+        eo[part] = total.astype(BF16)
         for m in range(m0, m0 + nm):
-            send_back(m)
-
-    def send_back(m):
+            send_back(core, m)
+
+    def send_back(core, m):
+        def peer(i):
+            n = lax.rem(half - core + i, jump)
+            source = eo.at[(core * 4 + m) * jump + n]
+            place = ret.at[m * slots + n * 2 + c]
+            where = {"ep": lax.rem(z - n + half - core + ring, ring), "tp": x, "dp": core}
+            return source, place, where
+
         def body(i, carry):
-            s = lax.rem(own + i, slots)
-            remote(
-                eo.at[m * slots + s],
-                ret.at[m * slots + lax.rem(s // 2 * 2 + c, slots)],
-                ts.at[m], tr.at[m], in_peer(s),
-            ).start()
+            source, place, where = peer(i)
+            remote(source, place, ts.at[m], tr.at[m], where).start()
             return carry
 
-        pltpu.make_async_copy(eo.at[m * slots + own], ret.at[m * slots + own], tr.at[m]).start()
-        lax.fori_loop(1, slots, body, 0)
+        source, place, where = peer(0)
+
+        @pl.when(c == core)
+        def _():
+            pltpu.make_async_copy(source, place, tr.at[m]).start()
+
+        @pl.when(c != core)
+        def _():
+            remote(source, place, ts.at[m], tr.at[m], where).start()
+
+        lax.fori_loop(1, jump, body, 0)
 
     def combine(m):
         part = pl.ds(m * slots, slots)
@@ -294,36 +352,40 @@
         quarters = both[0 : 4 * tok] + both[4 * tok :]
         return jnp.concatenate([quarters[q * tok : (q + 1) * tok] for q in range(4)], axis=1)
 
+    left, right = pl.ds(0, 2 * qw), pl.ds(2 * qw, 2 * qw)
+
     def k3_copies():
-        low, high = pl.ds(0, 2 * qw), pl.ds(2 * qw, 2 * qw)
         return [
-            remote(ksend.at[:, low], krecv.at[:, low], k3s.at[0], k3r.at[0], at_z(-jump)),
-            remote(ksend.at[:, high], krecv.at[:, high], k3s.at[1], k3r.at[1], at_z(jump)),
+            remote(ksend.at[:, left], krecv.at[:, left], k3s.at[0], k3r.at[0], at_z(-jump)),
+            remote(ksend.at[:, right], krecv.at[:, right], k3s.at[1], k3r.at[1], at_z(jump)),
         ]
 
-    def kf_copies():
-        return [
-            remote(fsend.at[0], frecv.at[0], kfs.at[0], kfr.at[0], at_z(-jump)),
-            remote(fsend.at[1], frecv.at[1], kfs.at[1], kfr.at[1], at_z(jump)),
-        ]
+    def kf_copy(i, number, part, where):
+        return remote(
+            fsend.at[number, :, part], frecv.at[number, :, part], kfs.at[i], kfr.at[i], at_z(where)
+        )
+
+    kf_copies = [
+        kf_copy(0, 0, right, -jump),
+        kf_copy(1, 1, left, jump),
+        kf_copy(2, 0, left, -jump),
+        kf_copy(3, 1, right, jump),
+    ]
 
     count = pack(0)
     send_local(0)
-    low, high = pl.ds(0, mid), pl.ds(mid, mid)
-    onward = [
-        remote(chunk.at[1, :, low], chunk.at[3, :, low], c3s.at[0], c3r.at[0], at_z(jump)),
-        remote(chunk.at[2, :, high], chunk.at[3, :, high], c3s.at[1], c3r.at[1], at_z(-jump)),
-    ]
     for first, second in zip(jumps, onward):
         first.wait_recv()
         second.start()
+    jumps[2].wait_recv()
     count = count + pack(1)
     send_local(1)
+    jumps[3].wait_recv()
     count = count + pack(2)
     send_local(2)
-    gather_1(0)
-    gather_2(0)
-    gather_1(1)
+    gather_1(N0)
+    gather_1(S0)
+    gather_1(N12)
     for copy in onward:
         copy.wait_recv()
     count = count + pack(3)
@@ -339,61 +401,67 @@
     pltpu.make_async_copy(cnt, crecv.at[own], nr).start()
     lax.fori_loop(1, slots, send_count, 0)
 
-    gather_2(1)
     for copy in weights:
         copy.wait()
-    ffn(0)
-    gather_1(2)
-    ffn(1)
-    gather_2(2)
-    reduce_1(0)
-    reduce_1(1)
-    reduce_2(0)
-    ffn(2)
-    reduce_2(1)
-
+    ffn(N0)
+    ffn(S0)
+    gather_2(N12)
+    gather_1(N3)
+    gather_1(S12)
+    gather_1(S3)
+    ffn(N12)
+    ffn(N3)
+    reduce_2(N0)
+    reduce_2(S0)
+    gather_2(S12)
+    reduce_1(N12)
+    ffn(S3)
+    ffn(S12)
+    reduce_2(N3)
+    reduce_2(N12)
     arrived(crecv, nr)
     csum[...] = jnp.sum(crecv[...], axis=0)
     count_1 = [
         remote(csum, cx.at[0], ncs.at[0], ncr.at[0], at_x(1)),
         remote(csum, cx.at[1], ncs.at[1], ncr.at[1], at_x(-1)),
+        remote(csum, cx.at[2], ncs.at[2], ncr.at[2], at_x(2)),
     ]
-    count_2 = remote(cx.at[0], cx.at[2], ncs.at[2], ncr.at[2], at_x(1))
     for copy in count_1:
         copy.start()
-
-    reduce_1(2)
-    count_1[0].wait_recv()
-    count_2.start()
+    reduce_2(S3)
+    reduce_1(S12)
     oparts[...] = combine(0)
-    reduce_2(2)
+
+    ksend[...] = combine(3).astype(BF16)
+    for copy in k3_copies():
+        copy.start()
+    reduce_2(S12)
     near = [combine(1), combine(2)]
-    count_1[1].wait_recv()
-    count_2.wait_recv()
+    fsend[0, :, 2 * qw :] = near[0][:, 2 * qw :].astype(BF16)
+    kf_copies[0].start()
+    fsend[1, :, 0 : 2 * qw] = near[1][:, 0 : 2 * qw].astype(BF16)
+    kf_copies[1].start()
+    for copy in count_1:
+        copy.wait_recv()
     total = csum[...] + cx[0] + cx[1] + cx[2]
     total = total[:, 0:experts] + total[:, experts:]
     loads[...] = total.astype(jnp.int32)
-
-    ksend[...] = combine(3).astype(BF16)
-    for copy in k3_copies():
-        copy.start()
-    first, second = k3_copies()
-    last = kf_copies()
-    first.wait_recv()
+    k3 = k3_copies()
+    k3[0].wait_recv()
     fsend[0, :, 0 : 2 * qw] = (near[0][:, 0 : 2 * qw] + krecv[:, 0 : 2 * qw].astype(F32)).astype(BF16)
-    fsend[0, :, 2 * qw :] = near[0][:, 2 * qw :].astype(BF16)
-    last[0].start()
-    second.wait_recv()
+    kf_copies[2].start()
+    k3[1].wait_recv()
     fsend[1, :, 2 * qw :] = (near[1][:, 2 * qw :] + krecv[:, 2 * qw :].astype(F32)).astype(BF16)
-    fsend[1, :, 0 : 2 * qw] = near[1][:, 0 : 2 * qw].astype(BF16)
-    last[1].start()
-    for copy in last:
+    kf_copies[3].start()
+    for copy in kf_copies:
         copy.wait_recv()
     out[...] = (oparts[...] + frecv[0].astype(F32) + frecv[1].astype(F32)).astype(BF16)
 
-    sends = jumps + onward + k3_copies() + last + count_1 + [count_2]
+    sends = jumps + onward + k3_copies() + kf_copies + count_1
     for g in range(len(GROUPS)):
-        sends += x1_copies(g) + x2_copies(g) + r1_copies(g) + r2_copies(g)
+        sends += x1_copies(g) + r1_copies(g) + r2_copies(g)
+        if g not in DIRECT:
+            sends += x2_copies(g)
     for copy in sends:
         copy.wait_send()
     for m in range(4):
@@ -417,11 +485,12 @@
     dma = pltpu.SemaphoreType.DMA
     block = (4 * slots, piece, qw)
     scratch = [
+        vmem((tok, width), BF16), vmem(expert_ids.shape[::-1], jnp.int32), vmem(gate_weights.shape[::-1], F32),
         vmem((width, hidden), BF16), vmem((width, hidden), BF16), vmem((width, hidden), BF16),
         vmem((4, tok, width + 2 * meta), BF16),
         vmem(block, BF16),
         vmem((4, *block), BF16),
-        vmem((qw // LANES, 2 * 4 * prow, LANES), F32),
+        vmem((qw // LANES, 4 * prow, LANES), F32),
         vmem((qw // LANES, 4 * 4 * prow, LANES), F32),
         vmem((3, *block), BF16),
         vmem(block, BF16), vmem(block, BF16), vmem(block, BF16), vmem(block, BF16),
@@ -432,11 +501,10 @@
         vmem((2, tok, width), BF16), vmem((2, tok, width), BF16),
         vmem((1, meta), F32), vmem((slots, 1, meta), F32),
         vmem((1, meta), F32), vmem((3, 1, meta), F32),
-        dma((3,)), dma((2,)), dma((2,)), dma((2,)), dma((2,)),
-        dma((4,)), dma((4,)),
+        dma((3,)), dma((3,)), dma((6,)), dma((6,)), dma((4,)), dma((8,)),
         dma((ng, 2)), dma((ng, 2)), dma((ng, 2)), dma((ng, 2)),
         dma((ng, 2)), dma((ng, 2)), dma((ng, 2)), dma((ng, 2)),
-        dma((4,)), dma((4,)), dma((2,)), dma((2,)), dma((2,)), dma((2,)),
+        dma((4,)), dma((4,)), dma((2,)), dma((2,)), dma((4,)), dma((4,)),
         dma(()), dma(()), dma((3,)), dma((3,)),
     ]
     in_vmem = pl.BlockSpec(memory_space=pltpu.VMEM)
@@ -447,14 +515,14 @@
             jax.ShapeDtypeStruct((tok, width), BF16),
             jax.ShapeDtypeStruct((1, experts), jnp.int32),
         ),
-        in_specs=[in_vmem, in_vmem, in_vmem, in_any, in_any, in_any],
+        in_specs=[in_any] * 6,
         out_specs=(in_vmem, in_vmem),
         scratch_shapes=scratch,
         compiler_params=pltpu.CompilerParams(
             collective_id=0, has_side_effects=True, vmem_limit_bytes=60 * 1024 * 1024
         ),
         name="routed_ffn",
-    )(tokens, expert_ids, gate_weights, w_gate[0], w_up[0], w_down[0])
+    )(tokens, expert_ids.T, gate_weights.T, w_gate[0], w_up[0], w_down[0])
     return mixed, loads[0]
 
 

time: 140 us -> 126 us (0.900)
  Pallas kernels: 133 us -> 122 us
  local copies, waits for them, and re-layouts: 5.25 us -> 2.57 us
    pallas_call x1, Pallas kernels: 133 us -> 122 us  [per_device(): pl.pallas_call(functools.partial(kernel, ring), out_shape=(jax.ShapeDtype...]
    unnamed x4 -> x2, local copies, waits for them, and re-layouts: 5.25 us -> 2.57 us
where the time goes in v2:
time: 126 us
  Pallas kernels  122 us (97%)
  local copies, waits for them, and re-layouts  2.57 us (2%)
    pallas_call x1, Pallas kernels, per_device(): pl.pallas_call(functools.partial(kernel, ring), out_shape=(jax.ShapeDtype...  122 us
    unnamed x2, local copies, waits for them, and re-layouts  2.57 us

profile of v2, /device:TPU:40, one launch (start us, length us, event | category | flops | bytes accessed | tf_op | source)
XLA Modules:
  0.0 125.6 jit_solution(15901096664321360133)
XLA Ops:
  0.6 122.4 %routed_ffn.1 = (bf16[16,1536]{1,0:T(8,128)(2,1)}, s32[1,64]{1,0:T(1,128)}) custom-call(bf16[16,1536]{1,0:T(8,128)(2,1)} %tokens_hbm.1, s32[4,16]{1,0:T(4,128)} %bitcast.9, f32[4,16]{1,0:T(4,128)} %bitcast.10, bf16[1536,384]{1,0:T(8,128)(2,1)} %bitcast.6, bf16[1536,384]{1,0:T(8,128)(2,1)} %bitcast.7, bf16[1536,384]{1,0:T(8,128)(2,1)} %bitcast.8), custom_call_target="tpu_custom_call" | custom-call | tf_op jit(solution)/shard_map/routed_ffn/pallas_call | solution.py:512
  123.0 1.4 %copy.10 = bf16[16,1536]{1,0:T(8,128)(2,1)} copy(bf16[16,1536]{1,0:T(8,128)(2,1)} %get-tuple-element.8) | data formatting | bytes 98304
  124.5 1.1 copy.11

commit v3 on v2

--- a/solution.py
+++ b/solution.py
@@ -94,17 +94,16 @@
 
     greet(at_z(jump))
     greet(at_z(-jump))
-
-    def greet_local(i, carry):
-        s = lax.rem(own + i, slots)
-        greet(out_peer(s))
-        greet(in_peer(s))
-        return carry
-
-    lax.fori_loop(1, slots, greet_local, 0)
-    greet(at_x(1))
-    greet(at_x(-1))
-    greet(at_x(2))
+    for d in (1, -1, 2):
+        greet(at_x(d))
+    greet({"ep": z, "tp": x, "dp": 1 - c})
+    for d in range(1, half):
+        for step in (d, -d):
+            for core in range(2):
+                greet({"ep": lax.rem(z + step + ring, ring), "tp": x, "dp": core})
+    greet({"ep": lax.rem(z + half, ring), "tp": x, "dp": 0})
+    greet({"ep": lax.rem(z - half + ring, ring), "tp": x, "dp": 1})
+    greet({"ep": lax.rem(z + (2 * c - 1) * half + ring, ring), "tp": x, "dp": c})
     for copy in weights:
         copy.start()
 
@@ -133,7 +132,7 @@
     chunk[0, :, mid : mid + 2 * qw] = tokens[:, 2 * qw :]
     chunk[0, :, mid + 2 * qw :] = gate_lo
 
-    pl.semaphore_wait(barrier, 2 * (slots - 1) + 5)
+    pl.semaphore_wait(barrier, 4 * half + 5)
 
     low, high = pl.ds(0, mid), pl.ds(mid, mid)
 
@@ -190,7 +189,7 @@
 
         here = xrecv.at[0, (c * 4 + m) * jump + own // 2]
         pltpu.make_async_copy(packed.at[m * slots + own], here, lr.at[c * 4 + m]).start()
-        lax.fori_loop(1, slots, body, 0)
+        lax.fori_loop(1, slots, body, 0, unroll=True)
 
     def span(g):
         core, m0, nm = GROUPS[g]
@@ -256,6 +255,11 @@
             for j in range(tiles):
                 place = pl.ds(4 * s0 * piece + q, rows, stride=4)
                 yf[j, place, :] = terms[:, j * LANES : (j + 1) * LANES]
+        if g not in (N0, S0):
+            spread(g)
+
+    def spread(g):
+        s0, n = span(g)
         part = pl.ds(s0, n)
         yb[1, part] = partial(g, 2, 0, n).astype(BF16)
         for copy in r1_copies(g):
@@ -342,7 +346,7 @@
         def _():
             remote(source, place, ts.at[m], tr.at[m], where).start()
 
-        lax.fori_loop(1, jump, body, 0)
+        lax.fori_loop(1, jump, body, 0, unroll=True)
 
     def combine(m):
         part = pl.ds(m * slots, slots)
@@ -377,13 +381,14 @@
     for first, second in zip(jumps, onward):
         first.wait_recv()
         second.start()
+    pl.when(c == 0)(lambda: gather_1(N0))
     jumps[2].wait_recv()
     count = count + pack(1)
     send_local(1)
     jumps[3].wait_recv()
     count = count + pack(2)
     send_local(2)
-    gather_1(N0)
+    pl.when(c != 0)(lambda: gather_1(N0))
     gather_1(S0)
     gather_1(N12)
     for copy in onward:
@@ -391,6 +396,20 @@
     count = count + pack(3)
     send_local(3)
 
+    gather_2(N12)
+    gather_1(S12)
+    gather_1(N3)
+    gather_1(S3)
+    for copy in weights:
+        copy.wait()
+    ffn(N0)
+    gather_2(S12)
+    ffn(N12)
+    ffn(N3)
+    ffn(S3)
+    ffn(S12)
+    ffn(S0)
+
     cnt[...] = count
 
     def send_count(i, carry):
@@ -401,24 +420,18 @@
     pltpu.make_async_copy(cnt, crecv.at[own], nr).start()
     lax.fori_loop(1, slots, send_count, 0)
 
-    for copy in weights:
-        copy.wait()
-    ffn(N0)
-    ffn(S0)
-    gather_2(N12)
-    gather_1(N3)
-    gather_1(S12)
-    gather_1(S3)
-    ffn(N12)
-    ffn(N3)
-    reduce_2(N0)
-    reduce_2(S0)
-    gather_2(S12)
     reduce_1(N12)
-    ffn(S3)
-    ffn(S12)
+    reduce_2(S3)
     reduce_2(N3)
+    reduce_1(S12)
+    spread(N0)
+    spread(S0)
     reduce_2(N12)
+    reduce_2(S12)
+
+    ksend[...] = combine(3).astype(BF16)
+    for copy in k3_copies():
+        copy.start()
     arrived(crecv, nr)
     csum[...] = jnp.sum(crecv[...], axis=0)
     count_1 = [
@@ -428,24 +441,13 @@
     ]
     for copy in count_1:
         copy.start()
-    reduce_2(S3)
-    reduce_1(S12)
-    oparts[...] = combine(0)
-
-    ksend[...] = combine(3).astype(BF16)
-    for copy in k3_copies():
-        copy.start()
-    reduce_2(S12)
+    reduce_2(N0)
+    reduce_2(S0)
     near = [combine(1), combine(2)]
     fsend[0, :, 2 * qw :] = near[0][:, 2 * qw :].astype(BF16)
     kf_copies[0].start()
     fsend[1, :, 0 : 2 * qw] = near[1][:, 0 : 2 * qw].astype(BF16)
     kf_copies[1].start()
-    for copy in count_1:
-        copy.wait_recv()
-    total = csum[...] + cx[0] + cx[1] + cx[2]
-    total = total[:, 0:experts] + total[:, experts:]
-    loads[...] = total.astype(jnp.int32)
     k3 = k3_copies()
     k3[0].wait_recv()
     fsend[0, :, 0 : 2 * qw] = (near[0][:, 0 : 2 * qw] + krecv[:, 0 : 2 * qw].astype(F32)).astype(BF16)
@@ -453,9 +455,15 @@
     k3[1].wait_recv()
     fsend[1, :, 2 * qw :] = (near[1][:, 2 * qw :] + krecv[:, 2 * qw :].astype(F32)).astype(BF16)
     kf_copies[3].start()
+    oparts[...] = combine(0)
+    for copy in count_1:
+        copy.wait_recv()
+    total = csum[...] + cx[0] + cx[1] + cx[2]
+    total = total[:, 0:experts] + total[:, experts:]
+    loads[...] = total
     for copy in kf_copies:
         copy.wait_recv()
-    out[...] = (oparts[...] + frecv[0].astype(F32) + frecv[1].astype(F32)).astype(BF16)
+    out[...] = oparts[...] + frecv[0].astype(F32) + frecv[1].astype(F32)
 
     sends = jumps + onward + k3_copies() + kf_copies + count_1
     for g in range(len(GROUPS)):
@@ -468,6 +476,11 @@
         arrived(packed.at[pl.ds(m * slots, slots - 1)], ls.at[m])
         arrived(eo.at[pl.ds(m * slots, slots - 1)], ts.at[m])
     arrived(crecv.at[pl.ds(0, slots - 1)], ns)
+
+
+def finish(sums, counts, mixed, loads):
+    mixed[...] = sums[...].astype(BF16)
+    loads[...] = counts[...].astype(jnp.int32)
 
 
 def per_device(tokens, expert_ids, gate_weights, w_gate, w_up, w_down):
@@ -509,11 +522,11 @@
     ]
     in_vmem = pl.BlockSpec(memory_space=pltpu.VMEM)
     in_any = pl.BlockSpec(memory_space=pl.ANY)
-    mixed, loads = pl.pallas_call(
+    sums, counts = pl.pallas_call(
         functools.partial(kernel, ring),
         out_shape=(
-            jax.ShapeDtypeStruct((tok, width), BF16),
-            jax.ShapeDtypeStruct((1, experts), jnp.int32),
+            jax.ShapeDtypeStruct((tok, width), F32),
+            jax.ShapeDtypeStruct((1, experts), F32),
         ),
         in_specs=[in_any] * 6,
         out_specs=(in_vmem, in_vmem),
@@ -523,6 +536,16 @@
         ),
         name="routed_ffn",
     )(tokens, expert_ids.T, gate_weights.T, w_gate[0], w_up[0], w_down[0])
+    mixed, loads = pl.pallas_call(
+        finish,
+        out_shape=(
+            jax.ShapeDtypeStruct((tok, width), BF16),
+            jax.ShapeDtypeStruct((1, experts), jnp.int32),
+        ),
+        in_specs=[in_vmem, in_vmem],
+        out_specs=(in_vmem, in_vmem),
+        name="finish",
+    )(sums, counts)
     return mixed, loads[0]
 
 

time: 126 us -> 124 us (0.984)
  local copies, waits for them, and re-layouts: 2.57 us -> 0 us
    unnamed x2 -> x0, local copies, waits for them, and re-layouts: 2.57 us -> none
    pallas_call x0 -> x1, Pallas kernels: none -> 1.52 us  [per_device(): pl.pallas_call(finish, out_shape=(jax.ShapeDtypeStruct((tok, width), BF16...]
where the time goes in v3:
time: 124 us
  Pallas kernels  123 us (99%)
    pallas_call x1, Pallas kernels, per_device(): pl.pallas_call(functools.partial(kernel, ring), out_shape=(jax.ShapeDtype...  121 us

profile of v3, /device:TPU:40, one launch (start us, length us, event | category | flops | bytes accessed | tf_op | source)
XLA Modules:
  0.0 123.6 jit_solution(4275918762291145612)
XLA Ops:
  0.6 121.4 %routed_ffn.1 = (f32[16,1536]{1,0:T(8,128)}, f32[1,64]{1,0:T(1,128)}) custom-call(bf16[16,1536]{1,0:T(8,128)(2,1)} %tokens_hbm.1, s32[4,16]{1,0:T(4,128)} %bitcast.9, f32[4,16]{1,0:T(4,128)} %bitcast.10, bf16[1536,384]{1,0:T(8,128)(2,1)} %bitcast.6, bf16[1536,384]{1,0:T(8,128)(2,1)} %bitcast.7, bf16[1536,384]{1,0:T(8,128)(2,1)} %bitcast.8), custom_call_target="tpu_custom_call" | custom-call | tf_op jit(solution)/shard_map/routed_ffn/pallas_call | solution.py:525
  122.1 1.5 %finish.1 = (bf16[16,1536]{1,0:T(8,128)(2,1)}, s32[1,64]{1,0:T(1,128)}) custom-call(f32[16,1536]{1,0:T(8,128)} %get-tuple-element.6.sums, f32[1,64]{1,0:T(1,128)} %get-tuple-element.7.counts), custom_call_target="tpu_custom_call" | custom-call | tf_op jit(solution)/shard_map/finish/pallas_call | solution.py:539

commit v4 on v3

--- a/solution.py
+++ b/solution.py
@@ -30,10 +30,10 @@
 
 
 def kernel(
-    ring, tokens_hbm, ids_hbm, gates_hbm, wg_hbm, wu_hbm, wd_hbm, out, loads,
-    tokens, ids, gates, wg, wu, wd, chunk, packed, xrecv, xf, yf, yb, ra, rb, sa, sb, eo, ret,
+    ring, tokens_hbm, ids_hbm, gates_hbm, wg_hbm, wu_hbm, wd_hbm, out_hbm, loads_hbm,
+    out, loads, tokens, ids, gates, wg, wu, wd, chunk, packed, xrecv, xf, yf, yb, ra, rb, sa, sb, eo, ret,
     gsel, oparts, ksend, krecv, fsend, frecv, cnt, crecv, csum, cx,
-    wsem, isem, cs, cr, ls, lr, x1s, x1r, x2s, x2r, r1s, r1r, r2s, r2r,
+    wsem, isem, osem, cs, cr, ls, lr, x1s, x1r, x2s, x2r, r1s, r1r, r2s, r2r,
     ts, tr, k3s, k3r, kfs, kfr, ns, nr, ncs, ncr,
 ):
     jump = ring // 4
@@ -202,20 +202,10 @@
     def x1_copies(g):
         s0, n = span(g)
         part = xrecv.at[0, pl.ds(s0, n)]
-        if g in DIRECT:
-            across = [remote(part, xrecv.at[2, pl.ds(s0, n)], x2s.at[g, 0], x2r.at[g, 0], at_x(2))]
-        else:
-            across = []
-        return across + [
+        return [
+            remote(part, xrecv.at[2, pl.ds(s0, n)], x2s.at[g, 0], x2r.at[g, 0], at_x(2)),
             remote(part, xrecv.at[1, pl.ds(s0, n)], x1s.at[g, 0], x1r.at[g, 0], at_x(1)),
             remote(part, xrecv.at[3, pl.ds(s0, n)], x1s.at[g, 1], x1r.at[g, 1], at_x(-1)),
-        ]
-
-    def x2_copies(g):
-        a, b = halves(g)
-        return [
-            remote(xrecv.at[1, a], xrecv.at[2, a], x2s.at[g, 0], x2r.at[g, 0], at_x(1)),
-            remote(xrecv.at[3, b], xrecv.at[2, b], x2s.at[g, 1], x2r.at[g, 1], at_x(-1)),
         ]
 
     def gather_1(g):
@@ -225,16 +215,11 @@
         for copy in x1_copies(g):
             copy.start()
 
-    def gather_2(g):
-        for one, two in zip(x1_copies(g), x2_copies(g)):
-            one.wait_recv()
-            two.start()
-
     def ffn(g):
         s0, n = span(g)
         count = 4 * n * piece
         rows = count // 4
-        for copy in x1_copies(g) if g in DIRECT else x2_copies(g):
+        for copy in x1_copies(g):
             copy.wait_recv()
         for j in range(tiles):
             arrivals = xrecv[:, pl.ds(s0, n), :, j * LANES : (j + 1) * LANES]
@@ -396,18 +381,18 @@
     count = count + pack(3)
     send_local(3)
 
-    gather_2(N12)
+    for copy in weights:
+        copy.wait()
+    ffn(N0)
     gather_1(S12)
     gather_1(N3)
     gather_1(S3)
-    for copy in weights:
-        copy.wait()
-    ffn(N0)
-    gather_2(S12)
     ffn(N12)
+    ffn(S12)
     ffn(N3)
     ffn(S3)
-    ffn(S12)
+    reduce_1(N12)
+    reduce_1(S12)
     ffn(S0)
 
     cnt[...] = count
@@ -420,10 +405,8 @@
     pltpu.make_async_copy(cnt, crecv.at[own], nr).start()
     lax.fori_loop(1, slots, send_count, 0)
 
-    reduce_1(N12)
     reduce_2(S3)
     reduce_2(N3)
-    reduce_1(S12)
     spread(N0)
     spread(S0)
     reduce_2(N12)
@@ -460,27 +443,31 @@
         copy.wait_recv()
     total = csum[...] + cx[0] + cx[1] + cx[2]
     total = total[:, 0:experts] + total[:, experts:]
-    loads[...] = total
+    loads[...] = total.astype(jnp.int32)
+    loads_out = pltpu.make_async_copy(loads, loads_hbm, osem.at[0])
+    loads_out.start()
     for copy in kf_copies:
         copy.wait_recv()
-    out[...] = oparts[...] + frecv[0].astype(F32) + frecv[1].astype(F32)
+    out[...] = (oparts[...] + frecv[0].astype(F32) + frecv[1].astype(F32)).astype(BF16)
+    mixed_out = pltpu.make_async_copy(out, out_hbm, osem.at[1])
+    mixed_out.start()
 
     sends = jumps + onward + k3_copies() + kf_copies + count_1
     for g in range(len(GROUPS)):
         sends += x1_copies(g) + r1_copies(g) + r2_copies(g)
-        if g not in DIRECT:
-            sends += x2_copies(g)
     for copy in sends:
         copy.wait_send()
     for m in range(4):
         arrived(packed.at[pl.ds(m * slots, slots - 1)], ls.at[m])
         arrived(eo.at[pl.ds(m * slots, slots - 1)], ts.at[m])
     arrived(crecv.at[pl.ds(0, slots - 1)], ns)
+    loads_out.wait()
+    mixed_out.wait()
 
 
 def finish(sums, counts, mixed, loads):
-    mixed[...] = sums[...].astype(BF16)
-    loads[...] = counts[...].astype(jnp.int32)
+    mixed[...] = sums[...]
+    loads[...] = counts[...]
 
 
 def per_device(tokens, expert_ids, gate_weights, w_gate, w_up, w_down):
@@ -498,6 +485,7 @@
     dma = pltpu.SemaphoreType.DMA
     block = (4 * slots, piece, qw)
     scratch = [
+        vmem((tok, width), BF16), vmem((1, experts), jnp.int32),
         vmem((tok, width), BF16), vmem(expert_ids.shape[::-1], jnp.int32), vmem(gate_weights.shape[::-1], F32),
         vmem((width, hidden), BF16), vmem((width, hidden), BF16), vmem((width, hidden), BF16),
         vmem((4, tok, width + 2 * meta), BF16),
@@ -514,7 +502,7 @@
         vmem((2, tok, width), BF16), vmem((2, tok, width), BF16),
         vmem((1, meta), F32), vmem((slots, 1, meta), F32),
         vmem((1, meta), F32), vmem((3, 1, meta), F32),
-        dma((3,)), dma((3,)), dma((6,)), dma((6,)), dma((4,)), dma((8,)),
+        dma((3,)), dma((3,)), dma((2,)), dma((6,)), dma((6,)), dma((4,)), dma((8,)),
         dma((ng, 2)), dma((ng, 2)), dma((ng, 2)), dma((ng, 2)),
         dma((ng, 2)), dma((ng, 2)), dma((ng, 2)), dma((ng, 2)),
         dma((4,)), dma((4,)), dma((2,)), dma((2,)), dma((4,)), dma((4,)),
@@ -525,11 +513,11 @@
     sums, counts = pl.pallas_call(
         functools.partial(kernel, ring),
         out_shape=(
-            jax.ShapeDtypeStruct((tok, width), F32),
-            jax.ShapeDtypeStruct((1, experts), F32),
+            jax.ShapeDtypeStruct((tok, width), BF16),
+            jax.ShapeDtypeStruct((1, experts), jnp.int32),
         ),
         in_specs=[in_any] * 6,
-        out_specs=(in_vmem, in_vmem),
+        out_specs=(in_any, in_any),
         scratch_shapes=scratch,
         compiler_params=pltpu.CompilerParams(
             collective_id=0, has_side_effects=True, vmem_limit_bytes=60 * 1024 * 1024

time: 124 us -> 124 us (level)
  no operation moved by 1% of the time
where the time goes in v4:
time: 124 us; the launch traced here: 123 us
  Pallas kernels  122 us (98%)
    pallas_call x1, Pallas kernels, per_device(): pl.pallas_call(functools.partial(kernel, ring), out_shape=(jax.ShapeDtype...  121 us

profile of v4, /device:TPU:40, one launch (start us, length us, event | category | flops | bytes accessed | tf_op | source)
XLA Modules:
  0.0 123.1 jit_solution(3018197020366071202)
XLA Ops:
  0.6 121.0 %routed_ffn.1 = (bf16[16,1536]{1,0:T(8,128)(2,1)}, s32[1,64]{1,0:T(1,128)}) custom-call(bf16[16,1536]{1,0:T(8,128)(2,1)} %tokens_hbm.1, s32[4,16]{1,0:T(4,128)} %bitcast.9, f32[4,16]{1,0:T(4,128)} %bitcast.10, bf16[1536,384]{1,0:T(8,128)(2,1)} %bitcast.6, bf16[1536,384]{1,0:T(8,128)(2,1)} %bitcast.7, bf16[1536,384]{1,0:T(8,128)(2,1)} %bitcast.8), custom_call_target="tpu_custom_call" | custom-call | tf_op jit(solution)/shard_map/routed_ffn/pallas_call | solution.py:513
  121.6 1.4 %finish.1 = (bf16[16,1536]{1,0:T(8,128)(2,1)}, s32[1,64]{1,0:T(1,128)}) custom-call(bf16[16,1536]{1,0:T(8,128)(2,1)} %get-tuple-element.6.sums, s32[1,64]{1,0:T(1,128)} %get-tuple-element.7.counts), custom_call_target="tpu_custom_call" | custom-call | tf_op jit(solution)/shard_map/finish/pallas_call | solution.py:527
